TPU v7x, 32 devices: a whole 2x2x4 slice. The times are simulated.
32 devices in a mesh: seq: 8 (over y, x, core), rep: 4 (over z).
Axes of the slice: x: 2, y: 2, z: 4, core: 2. Of those that a mesh axis runs over, the one named last changes fastest.
Arguments:
- query_rows: bfloat16 [8, 8, 256, 1152], P('rep', 'seq'), as said below
- key_rows: bfloat16 [8, 8, 256, 1152], P('rep', 'seq'), as said below
- value_rows: bfloat16 [8, 8, 256, 1152], P('rep', 'seq'), may hold values from -6 to 6
- out_grad: bfloat16 [8, 8, 256, 1152], P('rep', 'seq'), may hold values from -6 to 6
- out_weight: bfloat16 [1152, 1152], replicated, may hold values from -0.1875 to 0.1875
- frame_count: int32 [8], P('rep'), may hold values from 1 to 8, as said below
- pos_count: int32 [8], P('rep'), may hold values from 64 to 256, as said below
Outputs:
- projected: bfloat16 [8, 8, 256, 1152], P('rep', 'seq')
- grad_query: bfloat16 [8, 8, 256, 1152], P('rep', 'seq')
- grad_key: bfloat16 [8, 8, 256, 1152], P('rep', 'seq')
- grad_value: bfloat16 [8, 8, 256, 1152], P('rep', 'seq')
- grad_weight: float32 [1152, 1152], P('seq')
Inputs may be any that keep to these rules, and one draw needn't show every extreme that they name: `query_rows`: entries lie within -40 to 40. `key_rows`: entries lie within -40 to 40. `frame_count`: some clip has all 8 frames live. `pos_count`: some clip has all 256 positions live.
All inputs are finite; a program needn't handle non-finite values.
Results may differ from a plain program's by a relative error of at most 0.0057.
Values may be sent and summed in bfloat16 or wider, within the bound.
No kernel may reach another device: no remote copies, remote signals or barrier semaphores. Data moves between devices by JAX's collectives and lax.ppermute only.
A program may use at most 128 MiB of HBM per device.

v0:
```python
import math
import jax
import jax.numpy as jnp
from jax import lax
from jax.sharding import PartitionSpec as P

HEADS = 16


def attend_local(query_part, key_part, value_part, key_live, row_live):
    nframe, npos_part, width = query_part.shape
    head_dim = width // HEADS
    inv_root = 1.0 / math.sqrt(head_dim)
    shape_heads = (nframe, npos_part, HEADS, head_dim)
    query_heads = query_part.reshape(shape_heads)
    key_heads = key_part.reshape(shape_heads)
    value_heads = value_part.reshape(shape_heads)
    scores = (
        jnp.einsum("fphd,tphd->phft", query_heads, key_heads, preferred_element_type=jnp.float32)
        * inv_root
    )
    scores = jnp.where(key_live, scores, -1e30)
    highest = jnp.max(scores, axis=-1, keepdims=True)
    expo = jnp.exp(scores - highest) * key_live.astype(jnp.float32)
    weights = expo / jnp.sum(expo, axis=-1, keepdims=True)
    rounded = weights.astype(jnp.bfloat16)
    mixed = jnp.einsum("phft,tphd->fphd", rounded, value_heads, preferred_element_type=jnp.float32)
    attn_out = jnp.where(row_live[:, :, None], mixed.reshape(nframe, npos_part, width), 0.0).astype(
        jnp.bfloat16
    )
    return (attn_out, weights, rounded)


def attend_back(query_part, key_part, value_part, cot_part, weights, rounded):
    nframe, npos_part, width = query_part.shape
    head_dim = width // HEADS
    inv_root = 1.0 / math.sqrt(head_dim)
    shape_heads = (nframe, npos_part, HEADS, head_dim)
    cot_heads = cot_part.reshape(shape_heads)
    value_heads = value_part.reshape(shape_heads)
    grad_value = jnp.einsum(
        "phft,fphd->tphd", rounded, cot_heads, preferred_element_type=jnp.float32
    )
    grad_attn = jnp.einsum(
        "fphd,tphd->phft", cot_heads, value_heads, preferred_element_type=jnp.float32
    )
    row_delta = jnp.sum(weights * grad_attn, axis=-1, keepdims=True)
    grad_score = weights * (grad_attn - row_delta) * inv_root
    key_wide = key_part.astype(jnp.float32).reshape(shape_heads)
    query_wide = query_part.astype(jnp.float32).reshape(shape_heads)
    grad_query = jnp.einsum(
        "phft,tphd->fphd", grad_score, key_wide, precision=lax.Precision.HIGHEST
    )
    grad_key = jnp.einsum(
        "phft,fphd->tphd", grad_score, query_wide, precision=lax.Precision.HIGHEST
    )
    full = (nframe, npos_part, width)
    return (
        grad_query.reshape(full).astype(jnp.bfloat16),
        grad_key.reshape(full).astype(jnp.bfloat16),
        grad_value.reshape(full).astype(jnp.bfloat16),
    )


def reduce_weight(flat_grad, flat_out):
    mine = lax.psum_scatter(
        lax.dot_general(
            flat_grad, flat_out, (((0,), (0,)), ((), ())), preferred_element_type=jnp.float32
        ),
        "seq",
        scatter_dimension=0,
        tiled=True,
    )
    return lax.psum(mine, "rep")


def shards(query_rows, key_rows, value_rows, out_grad, out_weight, frame_count, pos_count):
    clip_local, frame_local, npos_all, width = query_rows.shape
    rank = lax.axis_index("seq")
    query_pos, key_pos, value_pos = (
        lax.all_to_all(query_rows, "seq", split_axis=2, concat_axis=1, tiled=True),
        lax.all_to_all(key_rows, "seq", split_axis=2, concat_axis=1, tiled=True),
        lax.all_to_all(value_rows, "seq", split_axis=2, concat_axis=1, tiled=True),
    )
    nframe = query_pos.shape[1]
    npos_part = query_pos.shape[2]
    frame_ids = jnp.arange(nframe, dtype=jnp.int32)
    position_ids = rank * npos_part + jnp.arange(npos_part, dtype=jnp.int32)
    key_live = frame_ids[None, :] < frame_count[:, None]
    row_live = key_live[:, :, None] & (position_ids[None, None, :] < pos_count[:, None, None])
    attn_pos, weights, rounded = jax.vmap(attend_local)(
        query_pos, key_pos, value_pos, key_live, row_live
    )
    attn_frames = lax.all_to_all(attn_pos, "seq", split_axis=1, concat_axis=2, tiled=True)
    flat_out = attn_frames.reshape(-1, width)
    flat_grad = out_grad.reshape(-1, width)
    projected = lax.dot_general(
        flat_out, out_weight, (((1,), (1,)), ((), ())), preferred_element_type=jnp.float32
    )
    projected = projected.astype(jnp.bfloat16).reshape(query_rows.shape)
    own_frames = rank * frame_local + jnp.arange(frame_local, dtype=jnp.int32)
    frame_alive = own_frames[None, :, None] < frame_count[:, None, None]
    place_alive = jnp.arange(npos_all, dtype=jnp.int32)[None, None, :] < pos_count[:, None, None]
    out_cot = jnp.dot(flat_grad, out_weight, preferred_element_type=jnp.float32).reshape(
        query_rows.shape
    )
    out_cot = jnp.where((frame_alive & place_alive)[..., None], out_cot, 0.0).astype(jnp.bfloat16)
    cot_pos = lax.all_to_all(out_cot, "seq", split_axis=2, concat_axis=1, tiled=True)
    grad_query_pos, grad_key_pos, grad_value_pos = jax.vmap(attend_back)(
        query_pos, key_pos, value_pos, cot_pos, weights, rounded
    )
    grad_query, grad_key, grad_value = (
        lax.all_to_all(grad_query_pos, "seq", split_axis=1, concat_axis=2, tiled=True),
        lax.all_to_all(grad_key_pos, "seq", split_axis=1, concat_axis=2, tiled=True),
        lax.all_to_all(grad_value_pos, "seq", split_axis=1, concat_axis=2, tiled=True),
    )
    grad_weight = reduce_weight(flat_grad, flat_out)
    return (projected, grad_query, grad_key, grad_value, grad_weight)


def solution(mesh):
    in_specs = (
        P("rep", "seq", None, None),
        P("rep", "seq", None, None),
        P("rep", "seq", None, None),
        P("rep", "seq", None, None),
        P(),
        P("rep"),
        P("rep"),
    )
    out_specs = (
        P("rep", "seq", None, None),
        P("rep", "seq", None, None),
        P("rep", "seq", None, None),
        P("rep", "seq", None, None),
        P("seq", None),
    )
    return jax.shard_map(shards, mesh=mesh, in_specs=in_specs, out_specs=out_specs, check_vma=False)
```

profile of v0, /device:TPU:0, one launch (start us, length us, event | category | flops | bytes accessed | tf_op | source)
XLA Modules:
  0.0 298.1 jit_solution(12987899901119479207)
XLA Ops:
  7.2 3.6 %copy.97 = bf16[2,1,256,1152]{3,0,1,2:T(2,128)(2,1)} copy(bf16[2,1,256,1152]{3,2,1,0:T(8,128)(2,1)} %param.7) | data formatting | bytes 2359296 | tf_op args[0]
  10.8 5.2 %all-to-all-start = ((bf16[2,1,256,1152]{3,0,1,2:T(2,128)(2,1)}), bf16[2,1,256,1152]{3,0,1,2:T(2,128)(2,1)}, u32[]{:S(2)}, u32[]{:S(2)}) async-start(bf16[2,1,256,1152]{3,0,1,2:T(2,128)(2,1)} %copy.97), calls=%async_computation | async-start | bytes 2359296 | tf_op jit(solution)/shard_map/all_to_all | solution.py:81
  16.0 3.5 %copy.99 = bf16[2,1,256,1152]{3,0,1,2:T(2,128)(2,1)} copy(bf16[2,1,256,1152]{3,2,1,0:T(8,128)(2,1)} %param.8) | data formatting | bytes 2359296 | tf_op args[1]
  19.5 13.4 %all-to-all-done = bf16[2,1,256,1152]{3,0,1,2:T(2,128)(2,1)} async-done(((bf16[2,1,256,1152]{3,0,1,2:T(2,128)(2,1)}), bf16[2,1,256,1152]{3,0,1,2:T(2,128)(2,1)}, u32[]{:S(2)}, u32[]{:S(2)}) %all-to-all-start) | async-done | bytes 1179680 | tf_op jit(solution)/shard_map/all_to_all | solution.py:81
  32.9 4.3 %all-to-all-start.1 = ((bf16[2,1,256,1152]{3,0,1,2:T(2,128)(2,1)}), bf16[2,1,256,1152]{3,0,1,2:T(2,128)(2,1)}, u32[]{:S(2)}, u32[]{:S(2)}) async-start(bf16[2,1,256,1152]{3,0,1,2:T(2,128)(2,1)} %copy.99), calls=%async_computation.1 | async-start | bytes 2359296 | tf_op jit(solution)/shard_map/all_to_all | solution.py:82
  37.2 3.5 %copy.103 = bf16[2,1,256,1152]{3,0,1,2:T(2,128)(2,1)} copy(bf16[2,1,256,1152]{3,2,1,0:T(8,128)(2,1)} %param.9) | data formatting | bytes 2359296 | tf_op args[2]
  40.7 13.3 %all-to-all-done.1 = bf16[2,1,256,1152]{3,0,1,2:T(2,128)(2,1)} async-done(((bf16[2,1,256,1152]{3,0,1,2:T(2,128)(2,1)}), bf16[2,1,256,1152]{3,0,1,2:T(2,128)(2,1)}, u32[]{:S(2)}, u32[]{:S(2)}) %all-to-all-start.1) | async-done | bytes 1179680 | tf_op jit(solution)/shard_map/all_to_all | solution.py:82
  54.0 4.2 %all-to-all-start.2 = ((bf16[2,1,256,1152]{3,0,1,2:T(2,128)(2,1)}), bf16[2,1,256,1152]{3,0,1,2:T(2,128)(2,1)}, u32[]{:S(2)}, u32[]{:S(2)}) async-start(bf16[2,1,256,1152]{3,0,1,2:T(2,128)(2,1)} %copy.103), calls=%async_computation.2 | async-start | bytes 2359296 | tf_op jit(solution)/shard_map/all_to_all | solution.py:83
  59.0 6.5 %reshape.214 = bf16[2,8,32,16,72]{4,3,0,2,1:T(8,128)(2,1)} reshape(bf16[2,1,256,1152]{3,0,1,2:T(2,128)(2,1)} %all-to-all-done) | data formatting | bytes 2359296 | tf_op jit(solution)/shard_map/vmap()/reshape | solution.py:15
  65.6 6.5 %reshape.215 = bf16[2,8,32,16,72]{4,3,0,2,1:T(8,128)(2,1)} reshape(bf16[2,1,256,1152]{3,0,1,2:T(2,128)(2,1)} %all-to-all-done.1) | data formatting | bytes 2359296 | tf_op jit(solution)/shard_map/vmap()/reshape | solution.py:16
  72.1 8.7 %fusion.38 = (f32[2,32,16,8]{3,2,1,0:T(8,128)S(1)}, f32[2,32,16,8,8]{3,4,2,1,0:T(8,128)}) fusion(f32[2,8]{1,0:T(2,128)S(1)} %get-tuple-element.31, pred[2,8]{1,0:T(4,128)(4,1)S(1)} %get-tuple-element.30, bf16[2,8,32,16,72]{4,3,0,2,1:T(8,128)(2,1)} %reshape.215, bf16[2,8,32,16,72]{4,3,0,2,1:T(8,128)(2,1)} %reshape.214), kind=kOutput, calls=%fused_computation.48 | convolution fusion | flops 9764871 | bytes 2654288 | tf_op jit(solution)/shard_map/vmap()/sub | solution.py:24
  80.8 6.5 %reshape.216 = bf16[2,8,32,16,72]{4,3,0,2,1:T(8,128)(2,1)} reshape(bf16[2,1,256,1152]{3,0,1,2:T(2,128)(2,1)} %all-to-all-done.2) | data formatting | bytes 2359296 | tf_op jit(solution)/shard_map/vmap()/reshape | solution.py:17
  87.3 4.1 %convolution_bitcast_fusion.1 = bf16[2,8,32,16,72]{4,1,3,2,0:T(8,128)(2,1)S(1)} fusion(bf16[2,8,32,16,72]{4,3,0,2,1:T(8,128)(2,1)} %reshape.216, f32[2,32,16,8,8]{3,4,2,1,0:T(8,128)} %get-tuple-element.33, f32[2,32,16,8]{3,2,1,0:T(8,128)S(1)} %get-tuple-element.32), kind=kOutput, calls=%fused_computation.13 | convolution fusion | flops 9568256 | bytes 2654208 | tf_op jit(solution)/shard_map/vmap(phft,tphd->fphd)/dot_general | solution.py:27
  93.1 4.6 %reshape.203 = bf16[2,8,32,1152]{3,2,1,0:T(8,128)(2,1)} reshape(bf16[2,8,32,16,72]{4,3,2,1,0:T(8,128)(2,1)} %copy.107) | data formatting | bytes 2359296 | tf_op jit(solution)/shard_map/vmap()/reshape | solution.py:28
  99.4 20.7 %all_to_all.81 = bf16[2,8,32,1152]{3,2,0,1:T(8,128)(2,1)S(1)} all-to-all(bf16[2,8,32,1152]{3,2,0,1:T(8,128)(2,1)S(1)} %copy.108), channel_id=1, replica_groups=mesh['seq'=8,'rep'=4] {'seq'}, dimensions={1} | all-to-all | bytes 2359296 | tf_op jit(solution)/shard_map/all_to_all | solution.py:94
  121.2 4.1 %convolution_bitcast_fusion = f32[1152,1152]{0,1:T(8,128)} fusion(bf16[512,1152]{1,0:T(8,128)(2,1)S(1)} %bitcast.59, bf16[512,1152]{1,0:T(8,128)(2,1)S(1)} %bitcast.64), kind=kOutput, calls=%fused_computation.1 | convolution fusion | flops 1358954496 | bytes 7667712 | tf_op jit(solution)/shard_map/dot_general | solution.py:67
  125.3 6.9 %copy.137 = f32[1152,1152]{1,0:T(8,128)} copy(f32[1152,1152]{0,1:T(8,128)} %convolution_bitcast_fusion) | data formatting | bytes 10616832
  132.3 3.1 %fusion.3 = bf16[2,1,256,1152]{3,2,0,1:T(8,128)(2,1)S(1)} fusion(bf16[1152,1152]{1,0:T(8,128)(2,1)S(1)} %copy-done, bf16[2,1,256,1152]{3,2,1,0:T(8,128)(2,1)} %param.10, pred[2,256]{1,0:T(4,128)(4,1)S(1)} %compare_and_fusion), kind=kOutput, calls=%fused_computation.10 | convolution fusion | flops 1360134144 | bytes 5014016 | tf_op jit(solution)/shard_map/dot_general | solution.py:104
  136.7 19.9 %all_to_all.82 = bf16[2,1,256,1152]{3,0,1,2:T(2,128)(2,1)} all-to-all(bf16[2,1,256,1152]{3,0,1,2:T(2,128)(2,1)S(1)} %copy.110), channel_id=1, replica_groups=mesh['seq'=8,'rep'=4] {'seq'}, dimensions={2} | all-to-all | bytes 2359296 | tf_op jit(solution)/shard_map/all_to_all | solution.py:108
  156.5 6.5 %reshape.217 = bf16[2,8,32,16,72]{4,3,0,2,1:T(8,128)(2,1)} reshape(bf16[2,1,256,1152]{3,0,1,2:T(2,128)(2,1)} %all_to_all.82) | data formatting | bytes 2359296 | tf_op jit(solution)/shard_map/vmap()/reshape | solution.py:39
  163.0 4.7 %convert_bitcast_fusion = bf16[2,8,32,16,72]{4,1,3,2,0:T(8,128)(2,1)S(1)} fusion(bf16[2,8,32,16,72]{4,3,0,2,1:T(8,128)(2,1)} %reshape.217, f32[2,32,16,8,8]{3,4,2,1,0:T(8,128)} %get-tuple-element.33, f32[2,32,16,8]{3,2,1,0:T(8,128)S(1)} %get-tuple-element.32), kind=kOutput, calls=%fused_computation.14 | convolution fusion | flops 10158080 | bytes 2654208 | tf_op jit(solution)/shard_map/vmap(phft,fphd->tphd)/dot_general | solution.py:41
  169.5 4.6 %reshape.211 = bf16[2,8,32,1152]{3,2,0,1:T(8,128)(2,1)} reshape(bf16[2,8,32,16,72]{4,3,2,0,1:T(8,128)(2,1)} %copy.136) | data formatting | bytes 2359296 | tf_op jit(solution)/shard_map/vmap()/convert_element_type | solution.py:61
  174.2 4.5 %all-to-all-start.7 = ((bf16[2,8,32,1152]{3,2,0,1:T(8,128)(2,1)}), bf16[2,8,32,1152]{3,2,0,1:T(8,128)(2,1)}, u32[]{:S(2)}, u32[]{:S(2)}) async-start(bf16[2,8,32,1152]{3,2,0,1:T(8,128)(2,1)} %reshape.211), calls=%async_computation.7 | async-start | bytes 2359296 | tf_op jit(solution)/shard_map/all_to_all | solution.py:115
  178.6 9.1 %multiply_reduce_fusion = (f32[2,32,16,8]{3,2,1,0:T(8,128)S(1)}, f32[2,32,16,8,8]{3,4,2,1,0:T(8,128)}) fusion(f32[2,32,16,8,8]{3,4,2,1,0:T(8,128)} %get-tuple-element.33, f32[2,32,16,8]{3,2,1,0:T(8,128)S(1)} %get-tuple-element.32, bf16[2,8,32,16,72]{4,3,0,2,1:T(8,128)(2,1)} %reshape.216, bf16[2,8,32,16,72]{4,3,0,2,1:T(8,128)(2,1)} %reshape.217), kind=kOutput, calls=%fused_computation.3 | convolution fusion | flops 9625600 | bytes 2949120 | tf_op jit(solution)/shard_map/vmap(fphd,tphd->phft)/dot_general | solution.py:44
  187.7 7.4 %convert_bitcast_fusion.1 = bf16[2,8,32,16,72]{4,1,3,2,0:T(8,128)(2,1)S(1)} fusion(bf16[2,8,32,16,72]{4,3,0,2,1:T(8,128)(2,1)S(1)} %copy-done.3, f32[2,32,16,8,8]{3,4,2,1,0:T(8,128)} %get-tuple-element.35, f32[2,32,16,8]{3,2,1,0:T(8,128)S(1)} %get-tuple-element.34, f32[2,32,16,8,8]{3,4,2,1,0:T(8,128)S(1)} %copy-done.7, ...), kind=kOutput, calls=%fused_computation.15 | convolution fusion | flops 57475072 | bytes 2949120 | tf_op jit(solution)/shard_map/vmap(phft,fphd->tphd)/dot_general | solution.py:54
  197.0 4.6 %reshape.210 = bf16[2,8,32,1152]{3,2,0,1:T(8,128)(2,1)} reshape(bf16[2,8,32,16,72]{4,3,2,0,1:T(8,128)(2,1)} %copy.135) | data formatting | bytes 2359296 | tf_op jit(solution)/shard_map/vmap()/convert_element_type | solution.py:60
  201.6 4.5 %all-to-all-start.6 = ((bf16[2,8,32,1152]{3,2,0,1:T(8,128)(2,1)}), bf16[2,8,32,1152]{3,2,0,1:T(8,128)(2,1)}, u32[]{:S(2)}, u32[]{:S(2)}) async-start(bf16[2,8,32,1152]{3,2,0,1:T(8,128)(2,1)} %reshape.210), calls=%async_computation.6 | async-start | bytes 2359296 | tf_op jit(solution)/shard_map/all_to_all | solution.py:114
  206.1 8.3 %convert_bitcast_fusion.2 = bf16[2,8,32,16,72]{4,1,3,2,0:T(8,128)(2,1)S(1)} fusion(bf16[2,8,32,16,72]{4,3,0,2,1:T(8,128)(2,1)} %reshape.215, f32[2,32,16,8,8]{3,4,2,1,0:T(8,128)} %get-tuple-element.35, f32[2,32,16,8]{3,2,1,0:T(8,128)} %copy-done.8, f32[2,32,16,8,8]{3,4,2,1,0:T(8,128)} %get-tuple-element.33, f32[2,32,16,8]{3,2,1,0:T(8,128)S(1)} %get-tuple-element.32), kind=kOutput, calls=%fused_computation.16 | convolution fusion | flops 57475072 | bytes 2949120 | tf_op jit(solution)/shard_map/vmap(phft,tphd->fphd)/dot_general | solution.py:51
  216.2 4.6 %reshape.209 = bf16[2,8,32,1152]{3,2,0,1:T(8,128)(2,1)} reshape(bf16[2,8,32,16,72]{4,3,2,0,1:T(8,128)(2,1)} %copy.134) | data formatting | bytes 2359296 | tf_op jit(solution)/shard_map/vmap()/convert_element_type | solution.py:59
  222.9 4.3 %all-to-all-start.5 = ((bf16[2,8,32,1152]{3,2,0,1:T(8,128)(2,1)}), bf16[2,8,32,1152]{3,2,0,1:T(8,128)(2,1)}, u32[]{:S(2)}, u32[]{:S(2)}) async-start(bf16[2,8,32,1152]{3,2,0,1:T(8,128)(2,1)} %reshape.209), calls=%async_computation.5 | async-start | bytes 2359296 | tf_op jit(solution)/shard_map/all_to_all | solution.py:113
  234.6 9.5 %all-to-all-done.5 = bf16[2,8,32,1152]{3,2,0,1:T(8,128)(2,1)} async-done(((bf16[2,8,32,1152]{3,2,0,1:T(8,128)(2,1)}), bf16[2,8,32,1152]{3,2,0,1:T(8,128)(2,1)}, u32[]{:S(2)}, u32[]{:S(2)}) %all-to-all-start.5) | async-done | bytes 1179680 | tf_op jit(solution)/shard_map/all_to_all | solution.py:113
  249.4 39.1 %all-reduce.2.cloned.1.call-done = f32[144,1152]{0,1:T(8,128)} async-done(((f32[144,1152]{0,1:T(8,128)}), f32[144,1152]{0,1:T(8,128)}) %all-reduce.2.cloned.1.call-update) | async-done | bytes 663568 | tf_op jit(solution)/shard_map/psum | solution.py:74
  (46 shorter events, 29.4 us)
Async XLA Ops:
  7.2 125.2 %copy-start = (bf16[1152,1152]{1,0:T(8,128)(2,1)S(1)}, bf16[1152,1152]{1,0:T(8,128)(2,1)}, u32[]{:S(2)}) copy-start(bf16[1152,1152]{1,0:T(8,128)(2,1)} %param.11) | copy-start | bytes 7962628
  10.8 22.1 %all-to-all-start = ((bf16[2,1,256,1152]{3,0,1,2:T(2,128)(2,1)}), bf16[2,1,256,1152]{3,0,1,2:T(2,128)(2,1)}, u32[]{:S(2)}, u32[]{:S(2)}) async-start(bf16[2,1,256,1152]{3,0,1,2:T(2,128)(2,1)} %copy.97), calls=%async_computation | async-start | bytes 2359296 | tf_op jit(solution)/shard_map/all_to_all | solution.py:81
  32.9 21.1 %all-to-all-start.1 = ((bf16[2,1,256,1152]{3,0,1,2:T(2,128)(2,1)}), bf16[2,1,256,1152]{3,0,1,2:T(2,128)(2,1)}, u32[]{:S(2)}, u32[]{:S(2)}) async-start(bf16[2,1,256,1152]{3,0,1,2:T(2,128)(2,1)} %copy.99), calls=%async_computation.1 | async-start | bytes 2359296 | tf_op jit(solution)/shard_map/all_to_all | solution.py:82
  37.2 21.6 %copy-start.6 = (s32[2]{0:T(128)S(1)}, s32[2]{0:T(128)}, u32[]{:S(2)}) copy-start(s32[2]{0:T(128)} %param.13) | copy-start | bytes 28
  37.2 21.7 %copy-start.5 = (s32[2]{0:T(128)S(1)}, s32[2]{0:T(128)}, u32[]{:S(2)}) copy-start(s32[2]{0:T(128)} %param.12) | copy-start | bytes 28
  54.0 26.8 %all-to-all-start.2 = ((bf16[2,1,256,1152]{3,0,1,2:T(2,128)(2,1)}), bf16[2,1,256,1152]{3,0,1,2:T(2,128)(2,1)}, u32[]{:S(2)}, u32[]{:S(2)}) async-start(bf16[2,1,256,1152]{3,0,1,2:T(2,128)(2,1)} %copy.103), calls=%async_computation.2 | async-start | bytes 2359296 | tf_op jit(solution)/shard_map/all_to_all | solution.py:83
  58.2 169.0 %reduce-scatter.4.cloned.1.call-start = ((), (), s32[]{:S(2)}) async-start(), calls=%async_computation.10 | async-start | bytes 5971968
  99.4 21.8 %copy-start.4 = (bf16[2,1,256,1152]{3,2,1,0:T(8,128)(2,1)S(1)}, bf16[2,1,256,1152]{3,2,1,0:T(8,128)(2,1)}, u32[]{:S(2)}) copy-start(bf16[2,1,256,1152]{3,2,1,0:T(8,128)(2,1)} %param.10) | copy-start | bytes 3538948
  120.2 1.0 copy-start.1
  174.2 27.5 %all-to-all-start.7 = ((bf16[2,8,32,1152]{3,2,0,1:T(8,128)(2,1)}), bf16[2,8,32,1152]{3,2,0,1:T(8,128)(2,1)}, u32[]{:S(2)}, u32[]{:S(2)}) async-start(bf16[2,8,32,1152]{3,2,0,1:T(8,128)(2,1)} %reshape.211), calls=%async_computation.7 | async-start | bytes 2359296 | tf_op jit(solution)/shard_map/all_to_all | solution.py:115
  178.6 9.1 %copy-start.3 = (bf16[2,8,32,16,72]{4,3,0,2,1:T(8,128)(2,1)S(1)}, bf16[2,8,32,16,72]{4,3,0,2,1:T(8,128)(2,1)}, u32[]{:S(2)}) copy-start(bf16[2,8,32,16,72]{4,3,0,2,1:T(8,128)(2,1)} %reshape.214) | copy-start | bytes 3538948
  178.6 9.1 %copy-start.7 = (f32[2,32,16,8,8]{3,4,2,1,0:T(8,128)S(1)}, f32[2,32,16,8,8]{3,4,2,1,0:T(8,128)}, u32[]{:S(2)}) copy-start(f32[2,32,16,8,8]{3,4,2,1,0:T(8,128)} %get-tuple-element.33) | copy-start | bytes 786436
  187.7 7.4 %copy-start.8 = (f32[2,32,16,8]{3,2,1,0:T(8,128)}, f32[2,32,16,8]{3,2,1,0:T(8,128)S(1)}, u32[]{:S(2)}) copy-start(f32[2,32,16,8]{3,2,1,0:T(8,128)S(1)} %get-tuple-element.34) | copy-start | bytes 98308
  201.6 21.3 %all-to-all-start.6 = ((bf16[2,8,32,1152]{3,2,0,1:T(8,128)(2,1)}), bf16[2,8,32,1152]{3,2,0,1:T(8,128)(2,1)}, u32[]{:S(2)}, u32[]{:S(2)}) async-start(bf16[2,8,32,1152]{3,2,0,1:T(8,128)(2,1)} %reshape.210), calls=%async_computation.6 | async-start | bytes 2359296 | tf_op jit(solution)/shard_map/all_to_all | solution.py:114
  222.9 21.1 %all-to-all-start.5 = ((bf16[2,8,32,1152]{3,2,0,1:T(8,128)(2,1)}), bf16[2,8,32,1152]{3,2,0,1:T(8,128)(2,1)}, u32[]{:S(2)}, u32[]{:S(2)}) async-start(bf16[2,8,32,1152]{3,2,0,1:T(8,128)(2,1)} %reshape.209), calls=%async_computation.5 | async-start | bytes 2359296 | tf_op jit(solution)/shard_map/all_to_all | solution.py:113
  227.2 61.3 %all-reduce.2.cloned.1.call-start = ((), (), s32[]{:S(2)}) async-start(), calls=%async_computation.9 | async-start | bytes 2359296 | tf_op jit(solution)/shard_map/psum | solution.py:74
  244.0 2.5 copy-start.2
Sparse Core Ops, SparseCore 0:
  132.3 65.9 reduce-scatter.3
  230.4 58.0 all-reduce.1
where the time goes:
time: 303 us; the launch traced here: 298 us
  local copies, waits for them, and re-layouts  83.8 us (28%)
  waiting for transfers between devices  77.4 us (26%)
  matrix products  52.4 us (17%)
  blocking collectives  40.6 us (13%)
  starting transfers between devices  27.5 us (9%)
  between operations  14.5 us (5%)
    psum x1, waiting for transfers between devices, reduce_weight(): return lax.psum(mine, 'rep')  39.1 us
    unnamed x24, local copies, waits for them, and re-layouts  23.5 us
    all_to_all x1, blocking collectives, shards(): lax.all_to_all(attn_pos, 'seq', split_axis=1, concat_axis=2, tiled=True)  20.7 us
    all_to_all x1, blocking collectives, shards(): lax.all_to_all(out_cot, 'seq', split_axis=2, concat_axis=1, tiled=True)  19.9 us
    all_to_all x1, waiting for transfers between devices, shards(): lax.all_to_all(query_rows, 'seq', split_axis=2, concat_axis=1, tiled=True)  13.4 us
    all_to_all x1, waiting for transfers between devices, shards(): lax.all_to_all(key_rows, 'seq', split_axis=2, concat_axis=1, tiled=True)  13.3 us
    all_to_all x1, waiting for transfers between devices, shards(): lax.all_to_all(grad_query_pos, 'seq', split_axis=1, concat_axis=2, tiled=...  9.45 us
    dot_general x1, matrix products, attend_back(): jnp.einsum('fphd,tphd->phft', cot_heads, value_heads, preferred_element_t...  9.06 us
  transfers between devices with their start and end apart: 8, of which 5 were waited for; matrix products, arithmetic and copies ran while one was open for 34% of the time, Pallas kernels for 0%

commit v1 on v0

--- a/solution.py
+++ b/solution.py
@@ -3,6 +3,7 @@
 import jax.numpy as jnp
 from jax import lax
 from jax.sharding import PartitionSpec as P
+from jax.lax import all_to_all, psum
 
 HEADS = 16
 
@@ -105,7 +106,10 @@
         query_rows.shape
     )
     out_cot = jnp.where((frame_alive & place_alive)[..., None], out_cot, 0.0).astype(jnp.bfloat16)
-    cot_pos = lax.all_to_all(out_cot, "seq", split_axis=2, concat_axis=1, tiled=True)
+    cot_pos = jnp.concatenate(
+        all_to_all(jnp.stack(jnp.split(out_cot, psum(1, "seq"), axis=2), axis=0), "seq", 0, 0),
+        axis=1,
+    )
     grad_query_pos, grad_key_pos, grad_value_pos = jax.vmap(attend_back)(
         query_pos, key_pos, value_pos, cot_pos, weights, rounded
     )

time: 303 us -> 334 us (1.10)
  waiting for transfers between devices: 77.4 us -> 95.8 us
  blocking collectives: 40.6 us -> 24.3 us
  local copies, waits for them, and re-layouts: 83.8 us -> 96.9 us
  matrix products: 52.4 us -> 64 us
  starting transfers between devices: 27.5 us -> 31.4 us
    all_to_all x2 -> x1, blocking collectives: 40.6 us -> 24.3 us  [shards(): all_to_all(jnp.stack(jnp.split(out_cot, psum(1, 'seq'), axis=2), axis=0),...]
    all_to_all x0 -> x1, waiting for transfers between devices: none -> 12 us  [shards(): lax.all_to_all(attn_pos, 'seq', split_axis=1, concat_axis=2, tiled=True)]
    unnamed x24 -> x31, local copies, waits for them, and re-layouts: 23.5 us -> 34.7 us
    dot_general x1, matrix products: 4.07 us -> 14.7 us  [attend_local(): jnp.einsum('phft,tphd->fphd', rounded, value_heads, preferred_element_typ...]
    all_to_all x1, waiting for transfers between devices: 0.01 us -> 9.43 us  [shards(): lax.all_to_all(grad_value_pos, 'seq', split_axis=1, concat_axis=2, tiled=...]
    another operation x0 -> x2, local copies, waits for them, and re-layouts: none -> 7.39 us  [the longest x1 5.79 us: attend_back(): cot_heads = cot_part.reshape(shape_heads)]
    reshape x1 -> x0, local copies, waits for them, and re-layouts: 6.53 us -> none  [attend_back(): cot_heads = cot_part.reshape(shape_heads)]
    all_to_all x0 -> x1, starting transfers between devices: none -> 4.26 us  [shards(): lax.all_to_all(attn_pos, 'seq', split_axis=1, concat_axis=2, tiled=True)]
  transfers between devices with their start and end apart: 8 -> 9, of which waited for: 5 -> 7; matrix products, arithmetic and copies ran while one was open for 34% -> 34% of each run, Pallas kernels for 0% -> 0%
where the time goes in v1:
time: 334 us; the launch traced here: 329 us
  local copies, waits for them, and re-layouts  96.9 us (29%)
  waiting for transfers between devices  95.8 us (29%)
  matrix products  64 us (19%)
  starting transfers between devices  31.4 us (9%)
  blocking collectives  24.3 us (7%)
  between operations  14.4 us (4%)
    psum x1, waiting for transfers between devices, reduce_weight(): return lax.psum(mine, 'rep')  40.1 us
    unnamed x31, local copies, waits for them, and re-layouts  34.7 us
    all_to_all x1, blocking collectives, shards(): all_to_all(jnp.stack(jnp.split(out_cot, psum(1, 'seq'), axis=2), axis=0),...  24.3 us
    dot_general x1, matrix products, attend_local(): jnp.einsum('phft,tphd->fphd', rounded, value_heads, preferred_element_typ...  14.7 us
    all_to_all x1, waiting for transfers between devices, shards(): lax.all_to_all(query_rows, 'seq', split_axis=2, concat_axis=1, tiled=True)  13.4 us
    all_to_all x1, waiting for transfers between devices, shards(): lax.all_to_all(key_rows, 'seq', split_axis=2, concat_axis=1, tiled=True)  13 us
    all_to_all x1, waiting for transfers between devices, shards(): lax.all_to_all(attn_pos, 'seq', split_axis=1, concat_axis=2, tiled=True)  12 us
    all_to_all x1, waiting for transfers between devices, shards(): lax.all_to_all(grad_value_pos, 'seq', split_axis=1, concat_axis=2, tiled=...  9.43 us
  transfers between devices with their start and end apart: 9, of which 7 were waited for; matrix products, arithmetic and copies ran while one was open for 34% of the time, Pallas kernels for 0%

profile of v1, /device:TPU:0, one launch (start us, length us, event | category | flops | bytes accessed | tf_op | source)
XLA Modules:
  0.0 328.6 jit_solution(11182204355906068811)
XLA Ops:
  7.2 3.6 %copy.96 = bf16[2,1,256,1152]{3,0,1,2:T(2,128)(2,1)} copy(bf16[2,1,256,1152]{3,2,1,0:T(8,128)(2,1)} %param.7) | data formatting | bytes 2359296 | tf_op args[0]
  10.8 5.2 %all-to-all-start = ((bf16[2,1,256,1152]{3,0,1,2:T(2,128)(2,1)}), bf16[2,1,256,1152]{3,0,1,2:T(2,128)(2,1)}, u32[]{:S(2)}, u32[]{:S(2)}) async-start(bf16[2,1,256,1152]{3,0,1,2:T(2,128)(2,1)} %copy.96), calls=%async_computation | async-start | bytes 2359296 | tf_op jit(solution)/shard_map/all_to_all | solution.py:82
  19.5 13.4 %all-to-all-done = bf16[2,1,256,1152]{3,0,1,2:T(2,128)(2,1)} async-done(((bf16[2,1,256,1152]{3,0,1,2:T(2,128)(2,1)}), bf16[2,1,256,1152]{3,0,1,2:T(2,128)(2,1)}, u32[]{:S(2)}, u32[]{:S(2)}) %all-to-all-start) | async-done | bytes 1179680 | tf_op jit(solution)/shard_map/all_to_all | solution.py:82
  32.9 4.3 %all-to-all-start.1 = ((bf16[2,1,256,1152]{3,0,1,2:T(2,128)(2,1)}), bf16[2,1,256,1152]{3,0,1,2:T(2,128)(2,1)}, u32[]{:S(2)}, u32[]{:S(2)}) async-start(bf16[2,1,256,1152]{3,0,1,2:T(2,128)(2,1)} %copy.98), calls=%async_computation.1 | async-start | bytes 2359296 | tf_op jit(solution)/shard_map/all_to_all | solution.py:83
  40.9 13.0 %all-to-all-done.1 = bf16[2,1,256,1152]{3,0,1,2:T(2,128)(2,1)} async-done(((bf16[2,1,256,1152]{3,0,1,2:T(2,128)(2,1)}), bf16[2,1,256,1152]{3,0,1,2:T(2,128)(2,1)}, u32[]{:S(2)}, u32[]{:S(2)}) %all-to-all-start.1) | async-done | bytes 1179680 | tf_op jit(solution)/shard_map/all_to_all | solution.py:83
  54.0 4.6 %all-to-all-start.2 = ((bf16[2,1,256,1152]{3,0,1,2:T(2,128)(2,1)}), bf16[2,1,256,1152]{3,0,1,2:T(2,128)(2,1)}, u32[]{:S(2)}, u32[]{:S(2)}) async-start(bf16[2,1,256,1152]{3,0,1,2:T(2,128)(2,1)} %copy.102), calls=%async_computation.2 | async-start | bytes 2359296 | tf_op jit(solution)/shard_map/all_to_all | solution.py:84
  58.7 4.1 %fusion.3 = bf16[2,1,256,1152]{3,2,0,1:T(8,128)(2,1)} fusion(bf16[1152,1152]{1,0:T(8,128)(2,1)S(1)} %copy-done, bf16[2,1,256,1152]{3,2,1,0:T(8,128)(2,1)} %param.10, pred[2,256]{1,0:T(4,128)(4,1)S(1)} %compare_and_fusion), kind=kOutput, calls=%fused_computation.10 | convolution fusion | flops 1360134144 | bytes 5014016 | tf_op jit(solution)/shard_map/dot_general | solution.py:105
  62.8 6.5 %reshape.210 = bf16[2,8,32,16,72]{4,3,0,2,1:T(8,128)(2,1)} reshape(bf16[2,1,256,1152]{3,0,1,2:T(2,128)(2,1)} %all-to-all-done) | data formatting | bytes 2359296 | tf_op jit(solution)/shard_map/vmap()/reshape | solution.py:16
  69.4 6.5 %reshape.211 = bf16[2,8,32,16,72]{4,3,0,2,1:T(8,128)(2,1)} reshape(bf16[2,1,256,1152]{3,0,1,2:T(2,128)(2,1)} %all-to-all-done.1) | data formatting | bytes 2359296 | tf_op jit(solution)/shard_map/vmap()/reshape | solution.py:17
  75.9 8.6 %fusion.46 = (f32[2,32,16,8]{3,2,1,0:T(8,128)S(1)}, f32[2,32,16,8,8]{3,4,2,1,0:T(8,128)}) fusion(f32[2,8]{1,0:T(2,128)S(1)} %get-tuple-element.31, pred[2,8]{1,0:T(4,128)(4,1)S(1)} %get-tuple-element.30, bf16[2,8,32,16,72]{4,3,0,2,1:T(8,128)(2,1)} %reshape.211, bf16[2,8,32,16,72]{4,3,0,2,1:T(8,128)(2,1)} %reshape.210), kind=kOutput, calls=%fused_computation.64 | convolution fusion | flops 9764871 | bytes 2654288 | tf_op jit(solution)/shard_map/vmap()/sub | solution.py:25
  84.5 6.5 %reshape.212 = bf16[2,8,32,16,72]{4,3,0,2,1:T(8,128)(2,1)} reshape(bf16[2,1,256,1152]{3,0,1,2:T(2,128)(2,1)} %all-to-all-done.2) | data formatting | bytes 2359296 | tf_op jit(solution)/shard_map/vmap()/reshape | solution.py:18
  91.0 14.7 %convolution_bitcast_fusion.1 = bf16[2,8,32,16,72]{4,1,3,2,0:T(8,128)(2,1)S(1)} fusion(bf16[2,8,32,16,72]{4,3,0,2,1:T(8,128)(2,1)} %reshape.212, f32[2,32,16,8,8]{3,4,2,1,0:T(8,128)} %get-tuple-element.33, f32[2,32,16,8]{3,2,1,0:T(8,128)S(1)} %get-tuple-element.32), kind=kOutput, calls=%fused_computation.13 | convolution fusion | flops 9568256 | bytes 2654208 | tf_op jit(solution)/shard_map/vmap(phft,tphd->fphd)/dot_general | solution.py:28
  107.5 4.6 %reshape.199 = bf16[2,8,32,1152]{3,2,1,0:T(8,128)(2,1)} reshape(bf16[2,8,32,16,72]{4,3,2,1,0:T(8,128)(2,1)} %copy.106) | data formatting | bytes 2359296 | tf_op jit(solution)/shard_map/vmap()/reshape | solution.py:29
  114.8 4.3 %all-to-all-start.3 = ((bf16[2,8,32,1152]{3,2,0,1:T(8,128)(2,1)}), bf16[2,8,32,1152]{3,2,0,1:T(8,128)(2,1)}, u32[]{:S(2)}, u32[]{:S(2)}) async-start(bf16[2,8,32,1152]{3,2,0,1:T(8,128)(2,1)} %copy.107), calls=%async_computation.3 | async-start | bytes 2359296 | tf_op jit(solution)/shard_map/all_to_all | solution.py:95
  123.9 12.0 %all-to-all-done.3 = bf16[2,8,32,1152]{3,2,0,1:T(8,128)(2,1)} async-done(((bf16[2,8,32,1152]{3,2,0,1:T(8,128)(2,1)}), bf16[2,8,32,1152]{3,2,0,1:T(8,128)(2,1)}, u32[]{:S(2)}, u32[]{:S(2)}) %all-to-all-start.3) | async-done | bytes 1179680 | tf_op jit(solution)/shard_map/all_to_all | solution.py:95
  138.3 4.1 %convolution_bitcast_fusion = f32[1152,1152]{0,1:T(8,128)} fusion(bf16[512,1152]{1,0:T(8,128)(2,1)S(1)} %bitcast.94, bf16[512,1152]{1,0:T(8,128)(2,1)S(1)} %bitcast.100), kind=kOutput, calls=%fused_computation.1 | convolution fusion | flops 1358954496 | bytes 7667712 | tf_op jit(solution)/shard_map/dot_general | solution.py:68
  142.4 6.9 %copy.134 = f32[1152,1152]{1,0:T(8,128)} copy(f32[1152,1152]{0,1:T(8,128)} %convolution_bitcast_fusion) | data formatting | bytes 10616832
  157.3 24.3 %all_to_all.77 = bf16[8,2,1,32,1152]{4,3,1,2,0:T(8,128)(2,1)} all-to-all(bf16[8,2,1,32,1152]{4,3,1,2,0:T(8,128)(2,1)} %fusion.33), channel_id=1, replica_groups=mesh['seq'=8,'rep'=4] {'seq'}, dimensions={0} | all-to-all | bytes 2359296 | tf_op jit(solution)/shard_map/all_to_all | solution.py:110
  181.5 5.8 %reshape_reshape.3 = bf16[2,8,32,16,72]{4,3,2,0,1:T(8,128)(2,1)} reshape(bf16[2,8,1,32,1152]{4,3,0,2,1:T(8,128)(2,1)} %bitcast.96) | data formatting | bytes 2359296 | tf_op jit(solution)/shard_map/vmap()/reshape;reshape | solution.py:40
  187.3 9.1 %multiply_reduce_fusion = (f32[2,32,16,8]{3,2,1,0:T(8,128)S(1)}, f32[2,32,16,8,8]{3,4,2,1,0:T(8,128)}) fusion(f32[2,32,16,8,8]{3,4,2,1,0:T(8,128)} %get-tuple-element.33, f32[2,32,16,8]{3,2,1,0:T(8,128)S(1)} %get-tuple-element.32, bf16[2,8,32,16,72]{4,3,0,2,1:T(8,128)(2,1)} %reshape.212, bf16[2,8,32,16,72]{4,3,2,0,1:T(8,128)(2,1)} %reshape_reshape.3), kind=kOutput, calls=%fused_computation.3 | convolution fusion | flops 9625600 | bytes 2949120 | tf_op jit(solution)/shard_map/vmap(fphd,tphd->phft)/dot_general | solution.py:45
  196.5 7.4 %convert_bitcast_fusion.1 = bf16[2,8,32,16,72]{4,1,3,2,0:T(8,128)(2,1)S(1)} fusion(bf16[2,8,32,16,72]{4,3,0,2,1:T(8,128)(2,1)S(1)} %copy-done.3, f32[2,32,16,8,8]{3,4,2,1,0:T(8,128)} %get-tuple-element.35, f32[2,32,16,8]{3,2,1,0:T(8,128)S(1)} %get-tuple-element.34, f32[2,32,16,8,8]{3,4,2,1,0:T(8,128)S(1)} %copy-done.7, ...), kind=kOutput, calls=%fused_computation.15 | convolution fusion | flops 57475072 | bytes 2949120 | tf_op jit(solution)/shard_map/vmap(phft,fphd->tphd)/dot_general | solution.py:55
  205.7 4.6 %reshape.206 = bf16[2,8,32,1152]{3,2,0,1:T(8,128)(2,1)} reshape(bf16[2,8,32,16,72]{4,3,2,0,1:T(8,128)(2,1)} %copy.132) | data formatting | bytes 2359296 | tf_op jit(solution)/shard_map/vmap()/convert_element_type | solution.py:61
  210.3 4.4 %all-to-all-start.6 = ((bf16[2,8,32,1152]{3,2,0,1:T(8,128)(2,1)}), bf16[2,8,32,1152]{3,2,0,1:T(8,128)(2,1)}, u32[]{:S(2)}, u32[]{:S(2)}) async-start(bf16[2,8,32,1152]{3,2,0,1:T(8,128)(2,1)} %reshape.206), calls=%async_computation.6 | async-start | bytes 2359296 | tf_op jit(solution)/shard_map/all_to_all | solution.py:118
  214.8 8.3 %convert_bitcast_fusion.2 = bf16[2,8,32,16,72]{4,1,3,2,0:T(8,128)(2,1)S(1)} fusion(bf16[2,8,32,16,72]{4,3,0,2,1:T(8,128)(2,1)} %reshape.211, f32[2,32,16,8,8]{3,4,2,1,0:T(8,128)} %get-tuple-element.35, f32[2,32,16,8]{3,2,1,0:T(8,128)} %copy-done.8, f32[2,32,16,8,8]{3,4,2,1,0:T(8,128)} %get-tuple-element.33, f32[2,32,16,8]{3,2,1,0:T(8,128)S(1)} %get-tuple-element.32), kind=kOutput, calls=%fused_computation.16 | convolution fusion | flops 57475072 | bytes 2949120 | tf_op jit(solution)/shard_map/vmap(phft,tphd->fphd)/dot_general | solution.py:52
  224.8 4.6 %reshape.205 = bf16[2,8,32,1152]{3,2,0,1:T(8,128)(2,1)} reshape(bf16[2,8,32,16,72]{4,3,2,0,1:T(8,128)(2,1)} %copy.131) | data formatting | bytes 2359296 | tf_op jit(solution)/shard_map/vmap()/convert_element_type | solution.py:60
  231.4 4.3 %all-to-all-start.5 = ((bf16[2,8,32,1152]{3,2,0,1:T(8,128)(2,1)}), bf16[2,8,32,1152]{3,2,0,1:T(8,128)(2,1)}, u32[]{:S(2)}, u32[]{:S(2)}) async-start(bf16[2,8,32,1152]{3,2,0,1:T(8,128)(2,1)} %reshape.205), calls=%async_computation.5 | async-start | bytes 2359296 | tf_op jit(solution)/shard_map/all_to_all | solution.py:117
  235.7 4.7 %convert_bitcast_fusion = bf16[2,8,32,16,72]{4,1,3,2,0:T(8,128)(2,1)S(1)} fusion(bf16[2,8,32,16,72]{4,3,2,0,1:T(8,128)(2,1)} %reshape_reshape.3, f32[2,32,16,8,8]{3,4,2,1,0:T(8,128)} %get-tuple-element.33, f32[2,32,16,8]{3,2,1,0:T(8,128)S(1)} %get-tuple-element.32), kind=kOutput, calls=%fused_computation.14 | convolution fusion | flops 10158080 | bytes 2654208 | tf_op jit(solution)/shard_map/vmap(phft,fphd->tphd)/dot_general | solution.py:42
  242.1 4.6 %reshape.207 = bf16[2,8,32,1152]{3,2,0,1:T(8,128)(2,1)} reshape(bf16[2,8,32,16,72]{4,3,2,0,1:T(8,128)(2,1)} %copy.133) | data formatting | bytes 2359296 | tf_op jit(solution)/shard_map/vmap()/convert_element_type | solution.py:62
  246.7 5.7 %all-to-all-done.5 = bf16[2,8,32,1152]{3,2,0,1:T(8,128)(2,1)} async-done(((bf16[2,8,32,1152]{3,2,0,1:T(8,128)(2,1)}), bf16[2,8,32,1152]{3,2,0,1:T(8,128)(2,1)}, u32[]{:S(2)}, u32[]{:S(2)}) %all-to-all-start.5) | async-done | bytes 1179680 | tf_op jit(solution)/shard_map/all_to_all | solution.py:117
  252.5 4.2 %all-to-all-start.7 = ((bf16[2,8,32,1152]{3,2,0,1:T(8,128)(2,1)}), bf16[2,8,32,1152]{3,2,0,1:T(8,128)(2,1)}, u32[]{:S(2)}, u32[]{:S(2)}) async-start(bf16[2,8,32,1152]{3,2,0,1:T(8,128)(2,1)} %reshape.207), calls=%async_computation.7 | async-start | bytes 2359296 | tf_op jit(solution)/shard_map/all_to_all | solution.py:119
  264.1 9.4 %all-to-all-done.7 = bf16[2,8,32,1152]{3,2,0,1:T(8,128)(2,1)} async-done(((bf16[2,8,32,1152]{3,2,0,1:T(8,128)(2,1)}), bf16[2,8,32,1152]{3,2,0,1:T(8,128)(2,1)}, u32[]{:S(2)}, u32[]{:S(2)}) %all-to-all-start.7) | async-done | bytes 1179680 | tf_op jit(solution)/shard_map/all_to_all | solution.py:119
  278.9 40.1 %all-reduce.2.cloned.1.call-done = f32[144,1152]{0,1:T(8,128)} async-done(((f32[144,1152]{0,1:T(8,128)}), f32[144,1152]{0,1:T(8,128)}) %all-reduce.2.cloned.1.call-update) | async-done | bytes 663568 | tf_op jit(solution)/shard_map/psum | solution.py:75
  (54 shorter events, 49.5 us)
Async XLA Ops:
  7.2 51.6 %copy-start = (bf16[1152,1152]{1,0:T(8,128)(2,1)S(1)}, bf16[1152,1152]{1,0:T(8,128)(2,1)}, u32[]{:S(2)}) copy-start(bf16[1152,1152]{1,0:T(8,128)(2,1)} %param.11) | copy-start | bytes 7962628
  10.8 22.1 %all-to-all-start = ((bf16[2,1,256,1152]{3,0,1,2:T(2,128)(2,1)}), bf16[2,1,256,1152]{3,0,1,2:T(2,128)(2,1)}, u32[]{:S(2)}, u32[]{:S(2)}) async-start(bf16[2,1,256,1152]{3,0,1,2:T(2,128)(2,1)} %copy.96), calls=%async_computation | async-start | bytes 2359296 | tf_op jit(solution)/shard_map/all_to_all | solution.py:82
  19.5 21.2 %copy-start.5 = (s32[2]{0:T(128)S(1)}, s32[2]{0:T(128)}, u32[]{:S(2)}) copy-start(s32[2]{0:T(128)} %param.12) | copy-start | bytes 28
  19.5 21.2 %copy-start.6 = (s32[2]{0:T(128)S(1)}, s32[2]{0:T(128)}, u32[]{:S(2)}) copy-start(s32[2]{0:T(128)} %param.13) | copy-start | bytes 28
  32.9 21.1 %all-to-all-start.1 = ((bf16[2,1,256,1152]{3,0,1,2:T(2,128)(2,1)}), bf16[2,1,256,1152]{3,0,1,2:T(2,128)(2,1)}, u32[]{:S(2)}, u32[]{:S(2)}) async-start(bf16[2,1,256,1152]{3,0,1,2:T(2,128)(2,1)} %copy.98), calls=%async_computation.1 | async-start | bytes 2359296 | tf_op jit(solution)/shard_map/all_to_all | solution.py:83
  54.0 30.5 %all-to-all-start.2 = ((bf16[2,1,256,1152]{3,0,1,2:T(2,128)(2,1)}), bf16[2,1,256,1152]{3,0,1,2:T(2,128)(2,1)}, u32[]{:S(2)}, u32[]{:S(2)}) async-start(bf16[2,1,256,1152]{3,0,1,2:T(2,128)(2,1)} %copy.102), calls=%async_computation.2 | async-start | bytes 2359296 | tf_op jit(solution)/shard_map/all_to_all | solution.py:84
  114.8 21.1 %all-to-all-start.3 = ((bf16[2,8,32,1152]{3,2,0,1:T(8,128)(2,1)}), bf16[2,8,32,1152]{3,2,0,1:T(8,128)(2,1)}, u32[]{:S(2)}, u32[]{:S(2)}) async-start(bf16[2,8,32,1152]{3,2,0,1:T(8,128)(2,1)} %copy.107), calls=%async_computation.3 | async-start | bytes 2359296 | tf_op jit(solution)/shard_map/all_to_all | solution.py:95
  119.1 137.7 %reduce-scatter.4.cloned.1.call-start = ((), (), s32[]{:S(2)}) async-start(), calls=%async_computation.10 | async-start | bytes 5971968
  135.9 2.5 copy-start.4
  137.3 1.0 copy-start.1
  187.3 9.2 %copy-start.3 = (bf16[2,8,32,16,72]{4,3,0,2,1:T(8,128)(2,1)S(1)}, bf16[2,8,32,16,72]{4,3,0,2,1:T(8,128)(2,1)}, u32[]{:S(2)}) copy-start(bf16[2,8,32,16,72]{4,3,0,2,1:T(8,128)(2,1)} %reshape.210) | copy-start | bytes 3538948
  187.3 9.2 %copy-start.7 = (f32[2,32,16,8,8]{3,4,2,1,0:T(8,128)S(1)}, f32[2,32,16,8,8]{3,4,2,1,0:T(8,128)}, u32[]{:S(2)}) copy-start(f32[2,32,16,8,8]{3,4,2,1,0:T(8,128)} %get-tuple-element.33) | copy-start | bytes 786436
  196.5 7.4 %copy-start.8 = (f32[2,32,16,8]{3,2,1,0:T(8,128)}, f32[2,32,16,8]{3,2,1,0:T(8,128)S(1)}, u32[]{:S(2)}) copy-start(f32[2,32,16,8]{3,2,1,0:T(8,128)S(1)} %get-tuple-element.34) | copy-start | bytes 98308
  210.3 21.1 %all-to-all-start.6 = ((bf16[2,8,32,1152]{3,2,0,1:T(8,128)(2,1)}), bf16[2,8,32,1152]{3,2,0,1:T(8,128)(2,1)}, u32[]{:S(2)}, u32[]{:S(2)}) async-start(bf16[2,8,32,1152]{3,2,0,1:T(8,128)(2,1)} %reshape.206), calls=%async_computation.6 | async-start | bytes 2359296 | tf_op jit(solution)/shard_map/all_to_all | solution.py:118
  231.4 21.1 %all-to-all-start.5 = ((bf16[2,8,32,1152]{3,2,0,1:T(8,128)(2,1)}), bf16[2,8,32,1152]{3,2,0,1:T(8,128)(2,1)}, u32[]{:S(2)}, u32[]{:S(2)}) async-start(bf16[2,8,32,1152]{3,2,0,1:T(8,128)(2,1)} %reshape.205), calls=%async_computation.5 | async-start | bytes 2359296 | tf_op jit(solution)/shard_map/all_to_all | solution.py:117
  252.5 21.1 %all-to-all-start.7 = ((bf16[2,8,32,1152]{3,2,0,1:T(8,128)(2,1)}), bf16[2,8,32,1152]{3,2,0,1:T(8,128)(2,1)}, u32[]{:S(2)}, u32[]{:S(2)}) async-start(bf16[2,8,32,1152]{3,2,0,1:T(8,128)(2,1)} %reshape.207), calls=%async_computation.7 | async-start | bytes 2359296 | tf_op jit(solution)/shard_map/all_to_all | solution.py:119
  256.7 62.3 %all-reduce.2.cloned.1.call-start = ((), (), s32[]{:S(2)}) async-start(), calls=%async_computation.9 | async-start | bytes 2359296 | tf_op jit(solution)/shard_map/psum | solution.py:75
  273.5 2.5 copy-start.2
Sparse Core Ops, SparseCore 0:
  149.4 60.1 reduce-scatter.3
  259.9 59.0 all-reduce.1
